TPU v7x, 32 devices: a whole 2x2x4 slice. The times are simulated.
32 devices in a mesh: dp: 8 (over z, core), tile: 4 (over y, x).
Axes of the slice: x: 2, y: 2, z: 4, core: 2. Of those that a mesh axis runs over, the one named last changes fastest.
Arguments:
- features: bfloat16 [8, 256, 512], P('dp', 'tile'), may hold values from -6 to 6
- depth_probs: float32 [8, 256, 118], P('dp', 'tile'), may hold values from 0 to 1, as said below
- context: bfloat16 [8, 256, 80], P('dp', 'tile'), may hold values from -2 to 2
- bev_grad: bfloat16 [8, 10240, 80], P('dp', 'tile'), may hold values from -18 to 18
- head_weight: bfloat16 [198, 512], replicated, may hold values from -0.4375 to 0.4375
- slot_cell: int32 [8, 4, 4, 512], P('dp', 'tile'), may hold values from 0 to 2559, as said below
- slot_point: int32 [8, 4, 4, 512], P('dp', 'tile'), may hold values from 0 to 7551, as said below
- slot_count: int32 [8, 4, 4], P('dp'), may hold values from 1 to 512, as said below
Outputs:
- grad_features: bfloat16 [8, 256, 512], P('dp', 'tile')
- head_weight_grad: float32 [512, 198], P('tile')
Inputs may be any that keep to these rules, and one draw needn't show every extreme that they name: `slot_count`: every block holds at most 512 live slots; in every scene group one tile receives exactly 512 from every device; the live slots of one device and group sum to at most 7552. `slot_point`: A live slot names a point of the sending device; within one group and sending device each point is named by at most one live slot; dead slots hold 0. `slot_cell`: A live slot names a cell of the receiving tile; dead slots hold 0. `depth_probs`: each pixel's 118 entries are positive and sum to one.
All inputs are finite; a program needn't handle non-finite values.
Results may differ from a plain program's by a relative error of at most 0.0049.
Values may be sent and summed in bfloat16 or wider, within the bound.
A program may use at most 64 MiB of HBM per device.

v0:
```python
import jax
import jax.numpy as jnp
from jax import lax
from jax.sharding import PartitionSpec as P


def lookup(bev_rows, cell_table):
    columns = jnp.arange(bev_rows.shape[0], dtype=jnp.int32)

    def cell_block(block_cells):
        one_hot = (block_cells[:, None] == columns[None, :]).astype(jnp.bfloat16)
        return jnp.dot(one_hot, bev_rows, preferred_element_type=jnp.float32).astype(jnp.bfloat16)

    return lax.map(cell_block, cell_table)


def slot_tables(points, pixels, depth_bins):
    flat_points = points.reshape(-1)
    pixel_of = flat_points // depth_bins
    bin_of = flat_points - pixel_of * depth_bins
    pixel_hot = (pixel_of[:, None] == jnp.arange(pixels, dtype=jnp.int32)[None, :]).astype(
        jnp.bfloat16
    )
    bin_hot = (bin_of[:, None] == jnp.arange(depth_bins, dtype=jnp.int32)[None, :]).astype(
        jnp.float32
    )
    return (pixel_hot, bin_hot)


def slot_probs(pixel_hot, bin_hot, depth_probs):
    spread = jnp.dot(
        pixel_hot.astype(jnp.float32),
        depth_probs,
        precision=lax.Precision.HIGHEST,
        preferred_element_type=jnp.float32,
    )
    return jnp.sum(spread * bin_hot, axis=-1)


def depth_from_slots(pixel_hot, bin_hot, slot_values):
    weighted = bin_hot * slot_values[:, None]
    return jnp.einsum(
        "kp,kd->pd",
        pixel_hot.astype(jnp.float32),
        weighted,
        precision=lax.Precision.HIGHEST,
        preferred_element_type=jnp.float32,
    )


def body(features, depth_probs, context, bev_grad, head_weight, slot_cell, slot_point, slot_count):
    own_index = lax.axis_index("tile")
    features = features[0]
    depth_probs = depth_probs[0]
    context = context[0]
    bev_rows = bev_grad[0]
    cell_table = slot_cell[0, 0]
    points = slot_point[0, 0]
    counts = slot_count[0]
    capacity = cell_table.shape[1]
    pixels, depth_bins = depth_probs.shape
    channels = context.shape[1]
    slot_ids = jnp.arange(capacity, dtype=jnp.int32)
    incoming = lax.dynamic_slice_in_dim(counts, own_index, 1, 1)[:, 0]
    live_in = slot_ids[None, :] < incoming[:, None]
    cell_values = jnp.where(
        live_in[..., None], lookup(bev_rows, cell_table), jnp.zeros((), jnp.bfloat16)
    )
    pixel_hot, bin_hot = slot_tables(points, pixels, depth_bins)
    prob_flat = slot_probs(pixel_hot, bin_hot, depth_probs)
    arrived = lax.all_to_all(cell_values, "tile", split_axis=0, concat_axis=0, tiled=True)
    arrived_flat = arrived.reshape(-1, channels).astype(jnp.float32)
    context_slot = jnp.dot(pixel_hot, context, preferred_element_type=jnp.float32)
    slot_grad = jnp.sum(arrived_flat * context_slot, axis=-1)
    grad_depth = depth_from_slots(pixel_hot, bin_hot, slot_grad)
    grad_ctx = jnp.einsum(
        "kp,kc->pc",
        pixel_hot.astype(jnp.float32),
        prob_flat[:, None] * arrived_flat,
        precision=lax.Precision.HIGHEST,
        preferred_element_type=jnp.float32,
    )
    grad_logits = depth_probs * (
        grad_depth - jnp.sum(depth_probs * grad_depth, axis=-1, keepdims=True)
    )
    head_grad = jnp.concatenate([grad_logits, grad_ctx], axis=-1).astype(jnp.bfloat16)
    grad_feats = jnp.dot(head_grad, head_weight, preferred_element_type=jnp.float32).astype(
        jnp.bfloat16
    )
    weight_share = lax.psum_scatter(
        jnp.dot(features.T, head_grad, preferred_element_type=jnp.float32),
        "tile",
        scatter_dimension=0,
        tiled=True,
    )
    summed = lax.psum(weight_share, "dp")
    return (grad_feats[None], summed)


def solution(mesh):
    return jax.shard_map(
        body,
        mesh=mesh,
        in_specs=(
            P("dp", "tile", None),
            P("dp", "tile", None),
            P("dp", "tile", None),
            P("dp", "tile", None),
            P(),
            P("dp", "tile", None, None),
            P("dp", "tile", None, None),
            P("dp", None, None),
        ),
        out_specs=(P("dp", "tile", None), P("tile", None)),
        check_vma=False,
    )
```

profile of v0, /device:TPU:0, one launch (start us, length us, event | category | flops | bytes accessed | tf_op | source)
XLA Modules:
  0.0 120.5 jit_solution(18162987026569552820)
XLA Ops:
  7.2 1.4 %copy.13 = bf16[1,2560,80]{2,1,0:T(8,128)(2,1)S(1)} copy(bf16[1,2560,80]{1,2,0:T(8,128)(2,1)} %param.13) | data formatting | bytes 819200 | tf_op args[3]
  8.6 7.8 %while.12 = (s32[]{:T(128)}, bf16[4,512,80]{1,2,0:T(8,128)(2,1)S(1)}, s32[4,512]{1,0:T(4,128)}, bf16[2560,80]{1,0:T(8,128)(2,1)S(1)}) while((s32[]{:T(128)}, bf16[4,512,80]{1,2,0:T(8,128)(2,1)S(1)}, s32[4,512]{1,0:T(4,128)}, bf16[2560,80]{1,0:T(8,128)(2,1)S(1)}) %tuple.39), condition=%wide.region_1.2_spmd.clone.clone, body=%wide.region_0.1_spmd.clone.sunk.clone | while | flops 211066880 | bytes 743493 | solution.py:14
  8.6 0.7 constant_dynamic-slice_fusion.3
  9.3 1.2 %fusion.40 = bf16[4,512,80]{1,2,0:T(8,128)(2,1)S(1)} fusion(bf16[4,512,80]{1,2,0:T(8,128)(2,1)S(1)} %get-tuple-element.92, s32[]{:T(128)S(6)} %copy.20, bf16[2560,80]{1,0:T(8,128)(2,1)S(1)} %get-tuple-element.98, s32[512]{0:T(512)S(1)} %bitcast.45), kind=kOutput, calls=%fused_computation.6.clone.1.clone | convolution fusion | flops 211066880 | bytes 739332 | tf_op jit(solution)/shard_map/while/body/eval_jaxpr/dot_general | solution.py:12
  10.5 0.7 constant_dynamic-slice_fusion.3
  11.3 1.2 %fusion.40 = bf16[4,512,80]{1,2,0:T(8,128)(2,1)S(1)} fusion(bf16[4,512,80]{1,2,0:T(8,128)(2,1)S(1)} %get-tuple-element.92, s32[]{:T(128)S(6)} %copy.20, bf16[2560,80]{1,0:T(8,128)(2,1)S(1)} %get-tuple-element.98, s32[512]{0:T(512)S(1)} %bitcast.45), kind=kOutput, calls=%fused_computation.6.clone.1.clone | convolution fusion | flops 211066880 | bytes 739332 | tf_op jit(solution)/shard_map/while/body/eval_jaxpr/dot_general | solution.py:12
  12.5 0.7 constant_dynamic-slice_fusion.3
  13.2 1.2 %fusion.40 = bf16[4,512,80]{1,2,0:T(8,128)(2,1)S(1)} fusion(bf16[4,512,80]{1,2,0:T(8,128)(2,1)S(1)} %get-tuple-element.92, s32[]{:T(128)S(6)} %copy.20, bf16[2560,80]{1,0:T(8,128)(2,1)S(1)} %get-tuple-element.98, s32[512]{0:T(512)S(1)} %bitcast.45), kind=kOutput, calls=%fused_computation.6.clone.1.clone | convolution fusion | flops 211066880 | bytes 739332 | tf_op jit(solution)/shard_map/while/body/eval_jaxpr/dot_general | solution.py:12
  14.5 0.7 constant_dynamic-slice_fusion.3
  15.2 1.2 %fusion.40 = bf16[4,512,80]{1,2,0:T(8,128)(2,1)S(1)} fusion(bf16[4,512,80]{1,2,0:T(8,128)(2,1)S(1)} %get-tuple-element.92, s32[]{:T(128)S(6)} %copy.20, bf16[2560,80]{1,0:T(8,128)(2,1)S(1)} %get-tuple-element.98, s32[512]{0:T(512)S(1)} %bitcast.45), kind=kOutput, calls=%fused_computation.6.clone.1.clone | convolution fusion | flops 211066880 | bytes 739332 | tf_op jit(solution)/shard_map/while/body/eval_jaxpr/dot_general | solution.py:12
  16.4 0.2 dynamic-slice_reduce_fusion
  16.7 0.7 broadcast_select_fusion
  17.4 5.2 %all-to-all-start = ((bf16[4,512,80]{1,2,0:T(8,128)(2,1)}), bf16[4,512,80]{1,2,0:T(8,128)(2,1)S(1)}, u32[]{:S(2)}, u32[]{:S(2)}) async-start(bf16[4,512,80]{1,2,0:T(8,128)(2,1)} %broadcast_select_fusion), calls=%async_computation | async-start | bytes 655360 | tf_op jit(solution)/shard_map/all_to_all | solution.py:71
  22.7 0.9 fusion.7
  23.6 4.9 %all-to-all-done = bf16[4,512,80]{1,2,0:T(8,128)(2,1)S(1)} async-done(((bf16[4,512,80]{1,2,0:T(8,128)(2,1)}), bf16[4,512,80]{1,2,0:T(8,128)(2,1)S(1)}, u32[]{:S(2)}, u32[]{:S(2)}) %all-to-all-start) | async-done | bytes 327712 | tf_op jit(solution)/shard_map/all_to_all | solution.py:71
  28.7 1.1 convolution_convert_fusion.1
  29.7 0.6 fusion.8
  30.3 1.3 %fusion.26 = (f32[64]{0:T(128)S(1)}, f32[64,118]{1,0:T(8,128)S(1)}) fusion(f32[1,64,118]{2,1,0:T(8,128)S(1)} %copy-done.2, f32[2048]{0:T(1024)S(1)} %fusion.8, s32[2048]{0:T(1024)S(1)} %get-tuple-element.48, s32[2048]{0:T(1024)S(1)} %get-tuple-element.49), kind=kOutput, calls=%fused_computation.37 | convolution fusion | flops 186358464 | bytes 85248 | tf_op jit(solution)/shard_map/kp,kd->pd/dot_general | solution.py:42
  31.6 0.1 fusion.27
  31.7 1.0 convolution_bitcast_fusion
  32.8 24.5 %reduce-scatter.2.cloned.1.call-done = f32[128,198]{0,1:T(8,128)} async-done(((f32[512,198]{0,1:T(8,128)}), f32[128,198]{0,1:T(8,128)}) %reduce-scatter.2.cloned.1.call-update) | async-done | bytes 101392 | tf_op jit(solution)/shard_map/reduce_scatter | solution.py:90
  57.3 0.8 fusion.9
  58.1 53.9 %all-reduce.2.cloned.1.call-done = f32[128,198]{0,1:T(8,128)} async-done(((f32[128,198]{0,1:T(8,128)}), f32[128,198]{0,1:T(8,128)}) %all-reduce.2.cloned.1.call-update) | async-done | bytes 101392 | tf_op jit(solution)/shard_map/psum | solution.py:96
  112.1 1.5 %copy.25 = f32[128,198]{0,1:T(8,128)} copy(f32[128,198]{0,1:T(8,128)} %all-reduce.2.cloned.1.call-done) | data formatting | bytes 202752
  (22 shorter events, 0.3 us)
Async XLA Ops:
  7.2 50.1 %copy-start = (bf16[198,512]{1,0:T(8,128)(2,1)S(1)}, bf16[198,512]{1,0:T(8,128)(2,1)}, u32[]{:S(2)}) copy-start(bf16[198,512]{1,0:T(8,128)(2,1)} %param.14) | copy-start | bytes 608260
  8.6 7.9 %copy-start.5 = (s32[1,4,4]{2,1,0:T(4,128)S(1)}, s32[1,4,4]{2,1,0:T(4,128)}, u32[]{:S(2)}) copy-start(s32[1,4,4]{2,1,0:T(4,128)} %param.17) | copy-start | bytes 196
  16.7 5.9 %copy-start.4 = (s32[1,1,4,512]{3,2,1,0:T(4,128)S(1)}, s32[1,1,4,512]{3,2,1,0:T(4,128)}, u32[]{:S(2)}) copy-start(s32[1,1,4,512]{3,2,1,0:T(4,128)} %param.16) | copy-start | bytes 24580
  16.7 6.0 %copy-start.2 = (f32[1,64,118]{2,1,0:T(8,128)S(1)}, f32[1,64,118]{2,1,0:T(8,128)}, u32[]{:S(2)}) copy-start(f32[1,64,118]{2,1,0:T(8,128)} %param.11) | copy-start | bytes 90628
  17.4 11.1 %all-to-all-start = ((bf16[4,512,80]{1,2,0:T(8,128)(2,1)}), bf16[4,512,80]{1,2,0:T(8,128)(2,1)S(1)}, u32[]{:S(2)}, u32[]{:S(2)}) async-start(bf16[4,512,80]{1,2,0:T(8,128)(2,1)} %broadcast_select_fusion), calls=%async_computation | async-start | bytes 655360 | tf_op jit(solution)/shard_map/all_to_all | solution.py:71
  22.6 34.6 %reduce-scatter.2.cloned.1.call-start = ((), (), s32[]{:S(2)}) async-start(), calls=%async_computation.2 | async-start | bytes 512000 | tf_op jit(solution)/shard_map/reduce_scatter | solution.py:90
  28.7 1.1 copy-start.3
  30.3 1.4 %copy-start.1 = (bf16[1,64,512]{2,1,0:T(8,128)(2,1)S(1)}, bf16[1,64,512]{2,1,0:T(8,128)(2,1)}, u32[]{:S(2)}) copy-start(bf16[1,64,512]{2,1,0:T(8,128)(2,1)} %param.10) | copy-start | bytes 196612
  32.7 79.3 %all-reduce.2.cloned.1.call-start = ((), (), s32[]{:S(2)}) async-start(), calls=%async_computation.3 | async-start | bytes 204800 | tf_op jit(solution)/shard_map/psum | solution.py:96
Sparse Core Ops, SparseCore 0:
  32.9 24.3 reduce-scatter.1
  59.6 52.4 all-reduce.1
where the time goes:
time: 121 us; the launch traced here: 120 us
  waiting for transfers between devices  83.4 us (69%)
  between operations  14.2 us (12%)
  matrix products  10.6 us (9%)
  local copies, waits for them, and re-layouts  6.01 us (5%)
  starting transfers between devices  5.24 us (4%)
    psum x1, waiting for transfers between devices, body(): summed = lax.psum(weight_share, 'dp')  53.9 us
    reduce_scatter x1, waiting for transfers between devices, body(): lax.psum_scatter(jnp.dot(features.T, head_grad, preferred_element_type=jn...  24.5 us
    all_to_all x1, starting transfers between devices, body(): lax.all_to_all(cell_values, 'tile', split_axis=0, concat_axis=0, tiled=True)  5.19 us
    dot_general x4, matrix products, cell_block(): jnp.dot(one_hot, bev_rows, preferred_element_type=jnp.float32)  4.93 us
    all_to_all x1, waiting for transfers between devices, body(): lax.all_to_all(cell_values, 'tile', split_axis=0, concat_axis=0, tiled=True)  4.91 us
    unnamed x15, local copies, waits for them, and re-layouts  2.94 us
    dynamic_slice x4, local copies, waits for them, and re-layouts, lookup(): return lax.map(cell_block, cell_table)  2.83 us
  transfers between devices with their start and end apart: 3, of which 3 were waited for; matrix products, arithmetic and copies ran while one was open for 1% of the time, Pallas kernels for 0%

commit v1 on v0

v1 whole, which is shorter than its diff:
```python
import functools

import jax
import jax.numpy as jnp
from jax import lax
from jax.experimental import pallas as pl
from jax.experimental.pallas import tpu as pltpu
from jax.sharding import PartitionSpec as P

F32 = jnp.float32
BF16 = jnp.bfloat16
MESH = pl.DeviceIdType.MESH
LANES = 128


def dot(a, b):
    return lax.dot_general(a, b, (((1,), (0,)), ((), ())), preferred_element_type=F32)


def dot_nt(a, b):
    return lax.dot_general(a, b, (((1,), (1,)), ((), ())), preferred_element_type=F32)


def eye(n):
    rows = lax.broadcasted_iota(jnp.int32, (n, n), 0)
    cols = lax.broadcasted_iota(jnp.int32, (n, n), 1)
    return (rows == cols).astype(BF16)


def transposed(x):
    return dot_nt(eye(x.shape[1]), x)


def kernel(
    dims,
    counts_ref,
    feat_ref,
    probs_ref,
    ctx_ref,
    bev_t,
    weight_ref,
    cell_ref,
    point_ref,
    gfeat_ref,
    gweight_ref,
    out_val,
    in_val,
    head_t,
    own_half,
    core_out,
    core_in,
    tile_out,
    tile_in,
    z_out,
    z_in,
    fin_out,
    fin_in,
    val_send,
    val_recv,
    core_send,
    core_recv,
    tile_send,
    tile_recv,
    z_send,
    z_recv,
    fin_send,
    fin_recv,
):
    tiles, pairs, half = dims
    me = lax.axis_index("tile")
    dp = lax.axis_index("dp")
    zi = dp // 2
    core = dp - zi * 2
    partner = zi * 2 + 1 - core

    def tile_peer(j):
        return (dp, lax.rem(me + j, tiles))

    def z_peer(j):
        return (lax.rem(zi + j, pairs) * 2 + core, me)

    barrier = pltpu.get_barrier_semaphore()
    for j in range(1, tiles):
        pl.semaphore_signal(barrier, inc=1, device_id=tile_peer(j), device_id_type=MESH)
    for j in range(1, pairs):
        pl.semaphore_signal(barrier, inc=1, device_id=z_peer(j), device_id_type=MESH)
    pl.semaphore_signal(barrier, inc=1, device_id=(partner, me), device_id_type=MESH)

    channels, cells = bev_t.shape
    cap = cell_ref.shape[1]
    pixels, bins = probs_ref.shape
    chunk = 512 if cells % 512 == 0 else cells
    lane = lax.broadcasted_iota(jnp.int32, (1, cap), 1)

    def lookup(j):
        dest = lax.rem(me + j, tiles)
        row = cell_ref[pl.ds(dest, 1), :]
        row = jnp.where(lane < counts_ref[dest, me], row, -1)
        total = jnp.zeros((channels, cap), F32)
        rows = lax.broadcasted_iota(jnp.int32, (chunk, cap), 0)
        for lo in range(0, cells, chunk):
            hot = (rows == row - lo).astype(BF16)
            total += dot(bev_t[:, lo : lo + chunk], hot)
        return total.astype(BF16)

    val_copies = []
    for j in range(1, tiles):
        out_val[j - 1] = lookup(j)
        if j == 1:
            pl.semaphore_wait(barrier, tiles + pairs - 1)
        copy = pltpu.make_async_remote_copy(
            src_ref=out_val.at[j - 1],
            dst_ref=in_val.at[j - 1],
            send_sem=val_send.at[j - 1],
            recv_sem=val_recv.at[j - 1],
            device_id=tile_peer(j),
            device_id_type=MESH,
        )
        copy.start()
        val_copies.append(copy)
    own_val = lookup(0)

    ctx_t = transposed(ctx_ref[...]).astype(BF16)
    probs = probs_ref[...]
    probs_hi = probs.astype(BF16)
    probs_lo = (probs - probs_hi.astype(F32)).astype(BF16)
    probs_hi_t = transposed(probs_hi)
    probs_t = probs_hi_t + transposed(probs_lo)
    probs_bt = probs_hi_t.astype(BF16)
    grad_depth = jnp.zeros((bins, pixels), F32)
    grad_ctx = jnp.zeros((channels, pixels), F32)
    pixel_rows = lax.broadcasted_iota(jnp.int32, (pixels, cap), 0)
    bin_rows = lax.broadcasted_iota(jnp.int32, (bins, cap), 0)
    for j in range(tiles):
        source = lax.rem(me + tiles - j, tiles)
        point = point_ref[pl.ds(source, 1), :].astype(F32)
        pixel = jnp.floor((point + 0.5) * (1.0 / bins))
        bin_of = (point - pixel * bins).astype(jnp.int32)
        pixel_hot = (pixel_rows == pixel.astype(jnp.int32)).astype(BF16)
        bin_hot = bin_rows == bin_of
        ctx_slot = dot(ctx_t, pixel_hot)
        prob_slot = jnp.sum(
            jnp.where(bin_hot, dot(probs_bt, pixel_hot), 0.0), axis=0, keepdims=True
        )
        if j:
            val_copies[j - 1].wait_recv()
            values = in_val[j - 1].astype(F32)
        else:
            values = own_val.astype(F32)
        slot_grad = jnp.sum(values * ctx_slot, axis=0, keepdims=True)
        spread = jnp.where(bin_hot, slot_grad, 0.0).astype(BF16)
        grad_depth += dot_nt(spread, pixel_hot)
        grad_ctx += dot_nt((values * prob_slot).astype(BF16), pixel_hot)

    mean = jnp.sum(probs_t * grad_depth, axis=0, keepdims=True)
    head_t[...] = jnp.zeros_like(head_t)
    head_t[0:bins, :] = probs_t * (grad_depth - mean)
    head_t[bins : bins + channels, :] = grad_ctx

    feats = feat_ref[...]
    share = feats.shape[1] // tiles
    other_head = head_t[pl.ds(pl.multiple_of((1 - core) * half, 8), half), :].astype(BF16)
    own_head = head_t[pl.ds(pl.multiple_of(core * half, 8), half), :].astype(BF16)
    product = dot(other_head, feats)
    for t in range(tiles):
        core_out[t] = product[:, t * share : (t + 1) * share].astype(BF16)
    core_copy = pltpu.make_async_remote_copy(
        src_ref=core_out,
        dst_ref=core_in,
        send_sem=core_send,
        recv_sem=core_recv,
        device_id=(partner, me),
        device_id_type=MESH,
    )
    core_copy.start()
    product = dot(own_head, feats)
    for t in range(tiles):
        own_half[t] = product[:, t * share : (t + 1) * share]
    core_copy.wait_recv()

    tile_copies = []
    for j in range(1, tiles):
        dest = lax.rem(me + j, tiles)
        tile_out[j - 1] = (own_half[dest] + core_in[dest].astype(F32)).astype(BF16)
        copy = pltpu.make_async_remote_copy(
            src_ref=tile_out.at[j - 1],
            dst_ref=tile_in.at[j - 1],
            send_sem=tile_send.at[j - 1],
            recv_sem=tile_recv.at[j - 1],
            device_id=tile_peer(j),
            device_id_type=MESH,
        )
        copy.start()
        tile_copies.append(copy)
    total = own_half[me] + core_in[me].astype(F32)

    head = dot_nt(eye(pixels), head_t[...].astype(BF16)).astype(BF16)
    outputs = bins + channels
    gfeat_ref[...] = dot(head[:, :outputs], weight_ref[...]).astype(BF16)

    for j in range(1, tiles):
        tile_copies[j - 1].wait_recv()
        total += tile_in[j - 1].astype(F32)
    z_copies = []
    z_out[...] = total.astype(BF16)
    for j in range(1, pairs):
        copy = pltpu.make_async_remote_copy(
            src_ref=z_out,
            dst_ref=z_in.at[j - 1],
            send_sem=z_send.at[j - 1],
            recv_sem=z_recv.at[j - 1],
            device_id=z_peer(j),
            device_id_type=MESH,
        )
        copy.start()
        z_copies.append(copy)
    for j in range(1, pairs):
        z_copies[j - 1].wait_recv()
        total += z_in[j - 1].astype(F32)
    fin_out[...] = total
    fin_copy = pltpu.make_async_remote_copy(
        src_ref=fin_out,
        dst_ref=fin_in,
        send_sem=fin_send,
        recv_sem=fin_recv,
        device_id=(partner, me),
        device_id_type=MESH,
    )
    fin_copy.start()
    gweight_ref[pl.ds(pl.multiple_of(core * half, 8), half), :] = total
    for copy in val_copies + [core_copy] + tile_copies + z_copies:
        copy.wait_send()
    fin_copy.wait()
    gweight_ref[pl.ds(pl.multiple_of((1 - core) * half, 8), half), :] = fin_in[...]


def body(tiles, dps, features, depth_probs, context, bev_grad, head_weight, slot_cell, slot_point, slot_count):
    features = features[0]
    depth_probs = depth_probs[0]
    context = context[0]
    bev_t = bev_grad[0].T
    cell_table = slot_cell[0, 0]
    points = slot_point[0, 0]
    counts = slot_count[0]
    cap = cell_table.shape[1]
    pixels, bins = depth_probs.shape
    channels = context.shape[1]
    inputs = features.shape[1]
    outputs = bins + channels
    pairs = dps // 2
    share = inputs // tiles
    half = -(-outputs // 32) * 16
    vmem = pl.BlockSpec(memory_space=pltpu.VMEM)
    dma = pltpu.SemaphoreType.DMA
    grad_feats, weight_t = pl.pallas_call(
        functools.partial(kernel, (tiles, pairs, half)),
        out_shape=(
            jax.ShapeDtypeStruct((pixels, inputs), BF16),
            jax.ShapeDtypeStruct((2 * half, share), F32),
        ),
        in_specs=[pl.BlockSpec(memory_space=pltpu.SMEM)] + [vmem] * 7,
        out_specs=(vmem, vmem),
        scratch_shapes=[
            pltpu.VMEM((tiles - 1, channels, cap), BF16),
            pltpu.VMEM((tiles - 1, channels, cap), BF16),
            pltpu.VMEM((2 * half, pixels), F32),
            pltpu.VMEM((tiles, half, share), F32),
            pltpu.VMEM((tiles, half, share), BF16),
            pltpu.VMEM((tiles, half, share), BF16),
            pltpu.VMEM((tiles - 1, half, share), BF16),
            pltpu.VMEM((tiles - 1, half, share), BF16),
            pltpu.VMEM((half, share), BF16),
            pltpu.VMEM((pairs - 1, half, share), BF16),
            pltpu.VMEM((half, share), F32),
            pltpu.VMEM((half, share), F32),
            dma((tiles - 1,)),
            dma((tiles - 1,)),
            dma,
            dma,
            dma((tiles - 1,)),
            dma((tiles - 1,)),
            dma((pairs - 1,)),
            dma((pairs - 1,)),
            dma,
            dma,
        ],
        compiler_params=pltpu.CompilerParams(collective_id=0, has_side_effects=True),
        name="splat_backward",
    )(counts, features, depth_probs, context, bev_t, head_weight, cell_table, points)
    return (grad_feats[None], weight_t[:outputs].T)


def solution(mesh):
    return jax.shard_map(
        functools.partial(body, mesh.shape["tile"], mesh.shape["dp"]),
        mesh=mesh,
        in_specs=(
            P("dp", "tile", None),
            P("dp", "tile", None),
            P("dp", "tile", None),
            P("dp", "tile", None),
            P(),
            P("dp", "tile", None, None),
            P("dp", "tile", None, None),
            P("dp", None, None),
        ),
        out_specs=(P("dp", "tile", None), P("tile", None)),
        check_vma=False,
    )
```

time: 121 us -> 25.3 us (0.21)
  waiting for transfers between devices: 83.4 us -> 0 us
  Pallas kernels: 0 us -> 22.3 us
  between operations: 14.2 us -> 0.65 us
  matrix products: 10.6 us -> 0 us
  starting transfers between devices: 5.24 us -> 0 us
  local copies, waits for them, and re-layouts: 6.01 us -> 2.21 us
    psum x1 -> x0, waiting for transfers between devices: 53.9 us -> none  [body(): summed = lax.psum(weight_share, 'dp')]
    reduce_scatter x1 -> x0, waiting for transfers between devices: 24.5 us -> none  [body(): lax.psum_scatter(jnp.dot(features.T, head_grad, preferred_element_type=jn...]
    pallas_call x0 -> x1, Pallas kernels: none -> 22.3 us  [body(): pl.pallas_call(functools.partial(kernel, (tiles, pairs, half)), out_shape...]
    dot_general x10 -> x0, matrix products: 10.6 us -> none  [the longest x4 4.93 us: cell_block(): jnp.dot(one_hot, bev_rows, preferred_element_type=jnp.float32)]
    all_to_all x1 -> x0, starting transfers between devices: 5.19 us -> none  [body(): lax.all_to_all(cell_values, 'tile', split_axis=0, concat_axis=0, tiled=True)]
    all_to_all x1 -> x0, waiting for transfers between devices: 4.91 us -> none  [body(): lax.all_to_all(cell_values, 'tile', split_axis=0, concat_axis=0, tiled=True)]
    dynamic_slice x5 -> x0, local copies, waits for them, and re-layouts: 3.01 us -> none  [the longest x4 2.83 us: lookup(): return lax.map(cell_block, cell_table)]
    unnamed x15 -> x3, local copies, waits for them, and re-layouts: 2.94 us -> 0.63 us
  transfers between devices with their start and end apart: 3 -> 0, of which waited for: 3 -> 0; matrix products, arithmetic and copies ran while one was open for 1% -> 0% of each run, Pallas kernels for 0% -> 0%
where the time goes in v1:
time: 25.3 us; the launch traced here: 25.1 us
  Pallas kernels  22.3 us (88%)
  local copies, waits for them, and re-layouts  2.21 us (9%)
  between operations  0.65 us (3%)
    pallas_call x1, Pallas kernels, body(): pl.pallas_call(functools.partial(kernel, (tiles, pairs, half)), out_shape...  22.3 us
    transpose x1, local copies, waits for them, and re-layouts, body(): return (grad_feats[None], weight_t[:outputs].T)  1.57 us
    unnamed x3, local copies, waits for them, and re-layouts  0.63 us

profile of v1, /device:TPU:0, one launch (start us, length us, event | category | flops | bytes accessed | tf_op | source)
XLA Modules:
  0.0 25.1 jit_solution(18203596139163038939)
XLA Ops:
  0.6 22.3 %splat_backward.1 = (bf16[64,512]{1,0:T(8,128)(2,1)}, f32[224,128]{1,0:T(8,128)}) custom-call(s32[4,4]{1,0:T(4,128)} %bitcast.19, bf16[64,512]{1,0:T(8,128)(2,1)} %bitcast.13, f32[64,118]{1,0:T(8,128)} %bitcast.15, bf16[64,80]{1,0:T(8,128)(2,1)} %bitcast.16, bf16[80,2560]{1,0:T(8,128)(2,1)} %bitcast.12, bf16[198,512]{1,0:T(8,128)(2,1)} %weight_ref.1, ...), custom_call_target="tpu_custom_call" | custom-call | tf_op jit(solution)/shard_map/splat_backward/pallas_call | solution.py:255
  22.9 0.0 copy-start
  22.9 1.6 %slice_bitcast_fusion = f32[128,198]{0,1:T(8,128)} fusion(f32[224,128]{1,0:T(8,128)} %get-tuple-element.5), kind=kLoop, calls=%fused_computation | loop fusion | bytes 202752 | tf_op jit(solution)/shard_map/transpose | solution.py:290
  24.5 0.0 copy-done
  24.5 0.6 %copy.11 = bf16[1,64,512]{2,1,0:T(8,128)(2,1)} copy(bf16[1,64,512]{2,1,0:T(8,128)(2,1)S(1)} %bitcast.14) | data formatting | bytes 131072
Async XLA Ops:
  22.9 1.6 %copy-start = (bf16[64,512]{1,0:T(8,128)(2,1)S(1)}, bf16[64,512]{1,0:T(8,128)(2,1)}, u32[]{:S(2)}) copy-start(bf16[64,512]{1,0:T(8,128)(2,1)} %get-tuple-element.4) | copy-start | bytes 196612

commit v2 on v1

--- a/solution.py
+++ b/solution.py
@@ -10,7 +10,6 @@
 F32 = jnp.float32
 BF16 = jnp.bfloat16
 MESH = pl.DeviceIdType.MESH
-LANES = 128
 
 
 def dot(a, b):
@@ -33,6 +32,16 @@
 
 def kernel(
     dims,
+    counts_hbm,
+    feat_hbm,
+    probs_hbm,
+    ctx_hbm,
+    bev_hbm,
+    weight_hbm,
+    cell_hbm,
+    point_hbm,
+    gfeat_ref,
+    gweight_ref,
     counts_ref,
     feat_ref,
     probs_ref,
@@ -41,8 +50,6 @@
     weight_ref,
     cell_ref,
     point_ref,
-    gfeat_ref,
-    gweight_ref,
     out_val,
     in_val,
     head_t,
@@ -55,6 +62,7 @@
     z_in,
     fin_out,
     fin_in,
+    load_sem,
     val_send,
     val_recv,
     core_send,
@@ -65,6 +73,8 @@
     z_recv,
     fin_send,
     fin_recv,
+    up_sem,
+    down_sem,
 ):
     tiles, pairs, half = dims
     me = lax.axis_index("tile")
@@ -72,30 +82,80 @@
     zi = dp // 2
     core = dp - zi * 2
     partner = zi * 2 + 1 - core
+    order = sorted(range(1, tiles), key=lambda j: -bin(j).count("1"))
+
+    def flipped(j):
+        index = 0
+        for place in range(tiles.bit_length() - 1):
+            bit = lax.rem(me // 2**place, 2)
+            index = index + 2**place * ((1 - bit) if (j >> place) & 1 else bit)
+        return index
 
     def tile_peer(j):
-        return (dp, lax.rem(me + j, tiles))
+        return (dp, flipped(j))
 
     def z_peer(j):
         return (lax.rem(zi + j, pairs) * 2 + core, me)
 
+    def z_step(by):
+        return ((zi + by) * 2 + core, me)
+
+    def signal(sem, device):
+        pl.semaphore_signal(sem, inc=1, device_id=device, device_id_type=MESH)
+
     barrier = pltpu.get_barrier_semaphore()
-    for j in range(1, tiles):
-        pl.semaphore_signal(barrier, inc=1, device_id=tile_peer(j), device_id_type=MESH)
-    for j in range(1, pairs):
-        pl.semaphore_signal(barrier, inc=1, device_id=z_peer(j), device_id_type=MESH)
-    pl.semaphore_signal(barrier, inc=1, device_id=(partner, me), device_id_type=MESH)
+    for j in order:
+        signal(barrier, tile_peer(j))
+    signal(barrier, (partner, me))
+
+    @pl.when(zi > 0)
+    def _():
+        signal(barrier, z_step(-1))
+
+    @pl.when(zi < pairs - 1)
+    def _():
+        signal(barrier, z_step(1))
+
+    loads = []
+    sources = (cell_hbm, counts_hbm, bev_hbm, point_hbm, ctx_hbm, probs_hbm, feat_hbm, weight_hbm)
+    targets = (cell_ref, counts_ref, bev_t, point_ref, ctx_ref, probs_ref, feat_ref, weight_ref)
+    for at, (src, dst) in enumerate(zip(sources, targets)):
+        load = pltpu.make_async_copy(src, dst, load_sem.at[at])
+        load.start()
+        loads.append(load)
+
+    def token_send(k):
+        @pl.when((zi < pairs - 1) & (zi >= k))
+        def _():
+            signal(up_sem.at[k - 1], z_step(1))
+
+        @pl.when((zi > 0) & (zi + k < pairs))
+        def _():
+            signal(down_sem.at[k - 1], z_step(-1))
+
+    def token_wait(k):
+        @pl.when(zi > k)
+        def _():
+            pl.semaphore_wait(up_sem.at[k - 1], 1)
+
+        @pl.when(zi + k + 1 < pairs)
+        def _():
+            pl.semaphore_wait(down_sem.at[k - 1], 1)
 
     channels, cells = bev_t.shape
     cap = cell_ref.shape[1]
     pixels, bins = probs_ref.shape
     chunk = 512 if cells % 512 == 0 else cells
     lane = lax.broadcasted_iota(jnp.int32, (1, cap), 1)
+    tile_lane = lax.broadcasted_iota(jnp.int32, (1, tiles), 1)
 
     def lookup(j):
-        dest = lax.rem(me + j, tiles)
+        dest = flipped(j)
         row = cell_ref[pl.ds(dest, 1), :]
-        row = jnp.where(lane < counts_ref[dest, me], row, -1)
+        live = jnp.sum(
+            jnp.where(tile_lane == me, counts_ref[pl.ds(dest, 1), :], 0), axis=1, keepdims=True
+        )
+        row = jnp.where(lane < live, row, -1)
         total = jnp.zeros((channels, cap), F32)
         rows = lax.broadcasted_iota(jnp.int32, (chunk, cap), 0)
         for lo in range(0, cells, chunk):
@@ -103,12 +163,10 @@
             total += dot(bev_t[:, lo : lo + chunk], hot)
         return total.astype(BF16)
 
-    val_copies = []
-    for j in range(1, tiles):
-        out_val[j - 1] = lookup(j)
-        if j == 1:
-            pl.semaphore_wait(barrier, tiles + pairs - 1)
-        copy = pltpu.make_async_remote_copy(
+    for load in loads[:3]:
+        load.wait()
+    val_copies = {
+        j: pltpu.make_async_remote_copy(
             src_ref=out_val.at[j - 1],
             dst_ref=in_val.at[j - 1],
             send_sem=val_send.at[j - 1],
@@ -116,10 +174,25 @@
             device_id=tile_peer(j),
             device_id_type=MESH,
         )
-        copy.start()
-        val_copies.append(copy)
+        for j in order
+    }
+    early = order[:2]
+    for j in early:
+        out_val[j - 1] = lookup(j)
+
+    beside = jnp.minimum(zi, 1) + jnp.minimum(pairs - 1 - zi, 1)
+    pl.semaphore_wait(barrier, tiles + beside)
+    for j in early:
+        val_copies[j].start()
+    if pairs > 2:
+        token_send(1)
+    for j in order[2:]:
+        out_val[j - 1] = lookup(j)
+        val_copies[j].start()
     own_val = lookup(0)
 
+    for load in loads[3:]:
+        load.wait()
     ctx_t = transposed(ctx_ref[...]).astype(BF16)
     probs = probs_ref[...]
     probs_hi = probs.astype(BF16)
@@ -131,24 +204,27 @@
     grad_ctx = jnp.zeros((channels, pixels), F32)
     pixel_rows = lax.broadcasted_iota(jnp.int32, (pixels, cap), 0)
     bin_rows = lax.broadcasted_iota(jnp.int32, (bins, cap), 0)
-    for j in range(tiles):
-        source = lax.rem(me + tiles - j, tiles)
-        point = point_ref[pl.ds(source, 1), :].astype(F32)
+    arrivals = [0] + order[::-1]
+    tables = {}
+    for j in arrivals:
+        point = point_ref[pl.ds(flipped(j), 1), :].astype(F32)
         pixel = jnp.floor((point + 0.5) * (1.0 / bins))
         bin_of = (point - pixel * bins).astype(jnp.int32)
         pixel_hot = (pixel_rows == pixel.astype(jnp.int32)).astype(BF16)
-        bin_hot = bin_rows == bin_of
         ctx_slot = dot(ctx_t, pixel_hot)
         prob_slot = jnp.sum(
-            jnp.where(bin_hot, dot(probs_bt, pixel_hot), 0.0), axis=0, keepdims=True
-        )
+            jnp.where(bin_rows == bin_of, dot(probs_bt, pixel_hot), 0.0), axis=0, keepdims=True
+        )
+        tables[j] = (bin_of, pixel_hot, ctx_slot, prob_slot)
+    for j in arrivals:
+        bin_of, pixel_hot, ctx_slot, prob_slot = tables[j]
         if j:
-            val_copies[j - 1].wait_recv()
+            val_copies[j].wait_recv()
             values = in_val[j - 1].astype(F32)
         else:
             values = own_val.astype(F32)
         slot_grad = jnp.sum(values * ctx_slot, axis=0, keepdims=True)
-        spread = jnp.where(bin_hot, slot_grad, 0.0).astype(BF16)
+        spread = jnp.where(bin_rows == bin_of, slot_grad, 0.0).astype(BF16)
         grad_depth += dot_nt(spread, pixel_hot)
         grad_ctx += dot_nt((values * prob_slot).astype(BF16), pixel_hot)
 
@@ -179,8 +255,8 @@
     core_copy.wait_recv()
 
     tile_copies = []
-    for j in range(1, tiles):
-        dest = lax.rem(me + j, tiles)
+    for j in order:
+        dest = flipped(j)
         tile_out[j - 1] = (own_half[dest] + core_in[dest].astype(F32)).astype(BF16)
         copy = pltpu.make_async_remote_copy(
             src_ref=tile_out.at[j - 1],
@@ -198,9 +274,13 @@
     outputs = bins + channels
     gfeat_ref[...] = dot(head[:, :outputs], weight_ref[...]).astype(BF16)
 
-    for j in range(1, tiles):
-        tile_copies[j - 1].wait_recv()
-        total += tile_in[j - 1].astype(F32)
+    for k in range(1, pairs - 1):
+        token_wait(k)
+        if k < pairs - 2:
+            token_send(k + 1)
+    for at in reversed(range(tiles - 1)):
+        tile_copies[at].wait_recv()
+        total += tile_in[order[at] - 1].astype(F32)
     z_copies = []
     z_out[...] = total.astype(BF16)
     for j in range(1, pairs):
@@ -227,11 +307,13 @@
         device_id_type=MESH,
     )
     fin_copy.start()
-    gweight_ref[pl.ds(pl.multiple_of(core * half, 8), half), :] = total
-    for copy in val_copies + [core_copy] + tile_copies + z_copies:
+    for copy in list(val_copies.values()) + [core_copy] + tile_copies + z_copies:
         copy.wait_send()
     fin_copy.wait()
-    gweight_ref[pl.ds(pl.multiple_of((1 - core) * half, 8), half), :] = fin_in[...]
+    other = fin_in[...]
+    first = core == 0
+    gweight_ref[0:half, :] = jnp.where(first, total, other)
+    gweight_ref[half:, :] = jnp.where(first, other, total)[: gweight_ref.shape[0] - half]
 
 
 def body(tiles, dps, features, depth_probs, context, bev_grad, head_weight, slot_cell, slot_point, slot_count):
@@ -250,17 +332,19 @@
     pairs = dps // 2
     share = inputs // tiles
     half = -(-outputs // 32) * 16
+    operands = (counts, features, depth_probs, context, bev_t, head_weight, cell_table, points)
     vmem = pl.BlockSpec(memory_space=pltpu.VMEM)
     dma = pltpu.SemaphoreType.DMA
     grad_feats, weight_t = pl.pallas_call(
         functools.partial(kernel, (tiles, pairs, half)),
         out_shape=(
             jax.ShapeDtypeStruct((pixels, inputs), BF16),
-            jax.ShapeDtypeStruct((2 * half, share), F32),
+            jax.ShapeDtypeStruct((outputs, share), F32),
         ),
-        in_specs=[pl.BlockSpec(memory_space=pltpu.SMEM)] + [vmem] * 7,
+        in_specs=[pl.BlockSpec(memory_space=pl.ANY)] * 8,
         out_specs=(vmem, vmem),
-        scratch_shapes=[
+        scratch_shapes=[pltpu.VMEM(a.shape, a.dtype) for a in operands]
+        + [
             pltpu.VMEM((tiles - 1, channels, cap), BF16),
             pltpu.VMEM((tiles - 1, channels, cap), BF16),
             pltpu.VMEM((2 * half, pixels), F32),
@@ -273,6 +357,7 @@
             pltpu.VMEM((pairs - 1, half, share), BF16),
             pltpu.VMEM((half, share), F32),
             pltpu.VMEM((half, share), F32),
+            dma((len(operands),)),
             dma((tiles - 1,)),
             dma((tiles - 1,)),
             dma,
@@ -283,11 +368,13 @@
             dma((pairs - 1,)),
             dma,
             dma,
+            pltpu.SemaphoreType.REGULAR((max(pairs - 2, 1),)),
+            pltpu.SemaphoreType.REGULAR((max(pairs - 2, 1),)),
         ],
         compiler_params=pltpu.CompilerParams(collective_id=0, has_side_effects=True),
         name="splat_backward",
-    )(counts, features, depth_probs, context, bev_t, head_weight, cell_table, points)
-    return (grad_feats[None], weight_t[:outputs].T)
+    )(*operands)
+    return (grad_feats[None], weight_t.T)
 
 
 def solution(mesh):

time: 25.3 us -> 25.6 us (1.012)
  Pallas kernels: 22.3 us -> 22.6 us
    transpose x1 -> x0, local copies, waits for them, and re-layouts: 1.57 us -> none  [body(): return (grad_feats[None], weight_t[:outputs].T)]
    unnamed x3 -> x4, local copies, waits for them, and re-layouts: 0.63 us -> 2.15 us
    pallas_call x1, Pallas kernels: 22.3 us -> 22.6 us  [body(): pl.pallas_call(functools.partial(kernel, (tiles, pairs, half)), out_shape...]
where the time goes in v2:
time: 25.6 us; the launch traced here: 25.4 us
  Pallas kernels  22.6 us (88%)
  local copies, waits for them, and re-layouts  2.15 us (8%)
  between operations  0.65 us (3%)
    pallas_call x1, Pallas kernels, body(): pl.pallas_call(functools.partial(kernel, (tiles, pairs, half)), out_shape...  22.6 us
    unnamed x4, local copies, waits for them, and re-layouts  2.15 us

profile of v2, /device:TPU:0, one launch (start us, length us, event | category | flops | bytes accessed | tf_op | source)
XLA Modules:
  0.0 25.4 jit_solution(3127320408957886607)
XLA Ops:
  0.6 22.6 %splat_backward.1 = (bf16[64,512]{1,0:T(8,128)(2,1)}, f32[198,128]{1,0:T(8,128)}) custom-call(s32[4,4]{1,0:T(4,128)} %bitcast.19, bf16[64,512]{1,0:T(8,128)(2,1)} %bitcast.13, f32[64,118]{1,0:T(8,128)} %bitcast.15, bf16[64,80]{1,0:T(8,128)(2,1)} %bitcast.16, bf16[80,2560]{1,0:T(8,128)(2,1)} %bitcast.11, bf16[198,512]{1,0:T(8,128)(2,1)} %weight_hbm.1, ...), custom_call_target="tpu_custom_call" | custom-call | tf_op jit(solution)/shard_map/splat_backward/pallas_call | solution.py:338
  23.2 0.0 copy-start
  23.2 1.5 %copy.12 = bf16[1,64,512]{2,1,0:T(8,128)(2,1)} copy(bf16[1,64,512]{2,1,0:T(8,128)(2,1)} %bitcast.14) | data formatting | bytes 131072
  24.7 0.0 copy-done
  24.7 0.6 %copy.13 = f32[128,198]{0,1:T(8,128)} copy(f32[128,198]{0,1:T(8,128)S(1)} %bitcast.12) | data formatting | bytes 202752
Async XLA Ops:
  23.2 1.5 %copy-start = (f32[198,128]{1,0:T(8,128)S(1)}, f32[198,128]{1,0:T(8,128)}, u32[]{:S(2)}) copy-start(f32[198,128]{1,0:T(8,128)} %get-tuple-element.5) | copy-start | bytes 304132

commit v3 on v2

--- a/solution.py
+++ b/solution.py
@@ -176,7 +176,7 @@
         )
         for j in order
     }
-    early = order[:2]
+    early = order[:1]
     for j in early:
         out_val[j - 1] = lookup(j)
 
@@ -186,7 +186,7 @@
         val_copies[j].start()
     if pairs > 2:
         token_send(1)
-    for j in order[2:]:
+    for j in order[1:]:
         out_val[j - 1] = lookup(j)
         val_copies[j].start()
     own_val = lookup(0)
@@ -338,8 +338,8 @@
     grad_feats, weight_t = pl.pallas_call(
         functools.partial(kernel, (tiles, pairs, half)),
         out_shape=(
-            jax.ShapeDtypeStruct((pixels, inputs), BF16),
-            jax.ShapeDtypeStruct((outputs, share), F32),
+            pltpu.VMEM((pixels, inputs), BF16),
+            pltpu.VMEM((outputs, share), F32),
         ),
         in_specs=[pl.BlockSpec(memory_space=pl.ANY)] * 8,
         out_specs=(vmem, vmem),

time: 25.6 us -> 23.6 us (0.922)
  Pallas kernels: 22.6 us -> 21.5 us
  local copies, waits for them, and re-layouts: 2.15 us -> 1.27 us
    pallas_call x1, Pallas kernels: 22.6 us -> 21.5 us  [body(): pl.pallas_call(functools.partial(kernel, (tiles, pairs, half)), out_shape...]
    unnamed x4 -> x2, local copies, waits for them, and re-layouts: 2.15 us -> 1.27 us
where the time goes in v3:
time: 23.6 us; the launch traced here: 23.4 us
  Pallas kernels  21.5 us (91%)
  local copies, waits for them, and re-layouts  1.27 us (5%)
  between operations  0.64 us (3%)
    pallas_call x1, Pallas kernels, body(): pl.pallas_call(functools.partial(kernel, (tiles, pairs, half)), out_shape...  21.5 us
    unnamed x2, local copies, waits for them, and re-layouts  1.27 us

profile of v3, /device:TPU:0, one launch (start us, length us, event | category | flops | bytes accessed | tf_op | source)
XLA Modules:
  0.0 23.4 jit_solution(12130698473731982234)
XLA Ops:
  0.6 21.5 %splat_backward.1 = (bf16[64,512]{1,0:T(8,128)(2,1)S(1)}, f32[198,128]{1,0:T(8,128)S(1)}) custom-call(s32[4,4]{1,0:T(4,128)} %bitcast.19, bf16[64,512]{1,0:T(8,128)(2,1)} %bitcast.14, f32[64,118]{1,0:T(8,128)} %bitcast.15, bf16[64,80]{1,0:T(8,128)(2,1)} %bitcast.16, bf16[80,2560]{1,0:T(8,128)(2,1)} %bitcast.13, bf16[198,512]{1,0:T(8,128)(2,1)} %weight_hbm.1, ...), custom_call_target="tpu_custom_call" | custom-call | tf_op jit(solution)/shard_map/splat_backward/pallas_call | solution.py:338
  22.1 0.6 %copy.12 = bf16[1,64,512]{2,1,0:T(8,128)(2,1)} copy(bf16[1,64,512]{2,1,0:T(8,128)(2,1)S(1)} %bitcast.12) | data formatting | bytes 131072
  22.8 0.6 %copy.13 = f32[128,198]{0,1:T(8,128)} copy(f32[128,198]{0,1:T(8,128)S(1)} %bitcast.11) | data formatting | bytes 202752
